TPU v7x, 32 devices: a whole 2x2x4 slice. The times are simulated.
32 devices in a mesh: rep: 2 (over x), span: 2 (over core), seq: 8 (over z, y).
Axes of the slice: x: 2, y: 2, z: 4, core: 2. Of those that a mesh axis runs over, the one named last changes fastest.
Arguments:
- queries: bfloat16 [4096, 2, 4096], P(('rep', 'span', 'seq')), parts along dimension 0, may hold values from -40 to 40
- keys: bfloat16 [4096, 2, 4096], P(('rep', 'span', 'seq')), parts along dimension 0, may hold values from -16 to 16
- values: bfloat16 [4096, 2, 4096], P(('rep', 'span', 'seq')), parts along dimension 0, may hold values from -6 to 6
- cache_keys: bfloat16 [1024, 2, 4096], P(('rep', 'span'), None, 'seq'), parts along dimension 0, may hold values from -9 to 9
- cache_values: bfloat16 [1024, 2, 4096], P(('rep', 'span'), None, 'seq'), parts along dimension 0, may hold values from -6 to 6
- span_lengths: int32 [4], P('rep'), parts along dimension 0, may hold values from 512 to 1024, as said below
- cache_offsets: int32 [4], P('rep'), parts along dimension 0, may hold values from 0 to 256
- step_index: int32 [4], P('rep'), parts along dimension 0, may hold values from 0 to 63
- step_gain: float32 [64, 4096], replicated, may hold values from -12 to 12
Outputs:
- attended: bfloat16 [4096, 2, 4096], P(('rep', 'span', 'seq')), parts along dimension 0
There are 2 independent parts, one for each index of `rep`. A program takes and returns all parts, laid end to end along the dimension named above; an argument that names none is the same for every part. Nothing has to cross between parts.
Inputs may be any that keep to these rules, and one draw needn't show every extreme that they name: `span_lengths`: at least one span has all 1024 tokens live; every span has at least 512.
All inputs are finite; a program needn't handle non-finite values.
Results may differ from a plain program's by a relative error of at most 0.015.
Values may be sent and summed in bfloat16 or wider, within the bound.
A program may use at most 128 MiB of HBM per device.

v0:
```python
import functools

import jax
import jax.numpy as jnp
from jax import lax
from jax.experimental import pallas as pl
from jax.experimental.pallas import tpu as pltpu
from jax.sharding import PartitionSpec as P

HD = 128
MESH = pl.DeviceIdType.MESH
masked_score = -1e30
KEYS, VALUES, QUERIES, OUTS = range(4)


def kernel(
    n_seq,
    n_span,
    q_ref,
    k_ref,
    v_ref,
    ck_ref,
    cv_ref,
    length_ref,
    offset_ref,
    step_ref,
    gain_ref,
    out_ref,
    kraw,
    vraw,
    qraw,
    oraw,
    ckraw,
    cvraw,
    kd,
    vd,
    qd,
    od,
    stage,
    bias,
    gain,
    row_gains,
    send_sem,
    recv_sem,
    cache_send,
    cache_recv,
    local_sem,
):
    n = n_seq * n_span
    seq, span = lax.axis_index("seq"), lax.axis_index("span")
    tokens, members, width = kraw.shape[1:]
    heads = width // HD
    piece = ckraw.shape[1]
    cached = n_span * piece
    scale = HD ** (-0.5)
    my_group = seq * n_span + span
    my_slot = span * n_seq + seq

    def ahead(k):
        return (
            lax.rem(seq + lax.div(k, n_span), n_seq),
            lax.rem(span + lax.rem(k, n_span), n_span),
        )

    def behind(k):
        return (
            lax.rem(seq + n_seq - lax.div(k, n_span), n_seq),
            lax.rem(span + n_span - lax.rem(k, n_span), n_span),
        )

    def nth(j):
        i = lax.div(j, n_span)
        swing = lax.div(i + 1, 2) * (2 * lax.rem(i, 2) - 1)
        lag = lax.rem(n_seq // 2 + swing + n_seq, n_seq)
        return lag * n_span + n_span - 1 - lax.rem(j, n_span)

    def columns(group):
        return pl.ds(pl.multiple_of(group * width, HD), width)

    def group_of(place):
        return place[0] * n_span + place[1]

    def slot_of(place):
        return place[1] * n_seq + place[0]

    def device(place):
        return {"seq": place[0], "span": place[1]}

    sources = (k_ref, v_ref, q_ref)
    landings = (kraw, vraw, qraw)

    def scatter(kind, k):
        to = ahead(k)
        return pltpu.make_async_remote_copy(
            src_ref=sources[kind].at[:, :, columns(group_of(to))],
            dst_ref=landings[kind].at[my_slot],
            send_sem=send_sem.at[kind, k],
            recv_sem=recv_sem.at[kind, k],
            device_id=device(to),
            device_id_type=MESH,
        )

    def arrival(kind, k):
        origin = behind(k)
        return pltpu.make_async_remote_copy(
            src_ref=sources[kind].at[:, :, columns(group_of(origin))],
            dst_ref=landings[kind].at[slot_of(origin)],
            send_sem=send_sem.at[kind, k],
            recv_sem=recv_sem.at[kind, k],
            device_id=device(origin),
            device_id_type=MESH,
        )

    def give_back(k):
        to = behind(k)
        return pltpu.make_async_remote_copy(
            src_ref=oraw.at[k],
            dst_ref=out_ref.at[:, :, columns(my_group)],
            send_sem=send_sem.at[OUTS, k],
            recv_sem=recv_sem.at[OUTS, k],
            device_id=device(to),
            device_id_type=MESH,
        )

    def returned(k):
        origin = ahead(k)
        return pltpu.make_async_remote_copy(
            src_ref=oraw.at[k],
            dst_ref=out_ref.at[:, :, columns(group_of(origin))],
            send_sem=send_sem.at[OUTS, k],
            recv_sem=recv_sem.at[OUTS, k],
            device_id=device(origin),
            device_id_type=MESH,
        )

    cache_pairs = ((ck_ref, ckraw), (cv_ref, cvraw))

    def cache_copy(which, b, to_span, from_span):
        source, landing = cache_pairs[which]
        return pltpu.make_async_remote_copy(
            src_ref=source.at[:, :, columns(to_span)],
            dst_ref=landing.at[from_span],
            send_sem=cache_send.at[which, b],
            recv_sem=cache_recv.at[which, b],
            device_id={"span": to_span},
            device_id_type=MESH,
        )

    own_copies = [
        pltpu.make_async_copy(
            sources[kind].at[:, :, columns(my_group)],
            landings[kind].at[my_slot],
            local_sem.at[kind],
        )
        for kind in range(3)
    ] + [
        pltpu.make_async_copy(
            cache_pairs[which][0].at[:, :, columns(span)],
            cache_pairs[which][1].at[span],
            local_sem.at[3 + which],
        )
        for which in range(2)
    ] + [
        pltpu.make_async_copy(gain_ref.at[:, columns(my_group)], gain, local_sem.at[5])
    ]

    barrier = pltpu.get_barrier_semaphore()

    @pl.loop(1, n)
    def _(k):
        pl.semaphore_signal(barrier, inc=1, device_id=device(ahead(k)), device_id_type=MESH)

    for copy in own_copies:
        copy.start()
    pl.semaphore_wait(barrier, n - 1)

    for b in range(1, n_span):
        for which in range(2):
            cache_copy(which, b, lax.rem(span + b, n_span), span).start()
    for kind in range(3):

        @pl.loop(0, n - 1)
        def _(j, kind=kind):
            scatter(kind, nth(j)).start()

    def separate(block, target, row):
        for h in range(heads):
            stage[h] = (
                block[:, :, h * HD : (h + 1) * HD].reshape(members * tokens, HD).astype(jnp.float32)
            )
            for m in range(members):
                target[h * members + m, pl.ds(row, tokens), :] = stage[
                    h, pl.ds(m, tokens, stride=members), :
                ].astype(jnp.bfloat16)

    span_len = n_seq * tokens
    places = lax.broadcasted_iota(jnp.int32, (1, cached), 1)
    live = lax.broadcasted_iota(jnp.int32, (1, span_len), 1)
    for c in range(n_span):
        bias[c : c + 1, 0:cached] = jnp.where(places >= offset_ref[c], 0.0, masked_score)
        for e in range(c + 1):
            first = cached + e * span_len
            bias[c : c + 1, first : first + span_len] = jnp.where(
                live < length_ref[e], 0.0, masked_score
            )
    for copy in own_copies:
        copy.wait()
    levels = lax.broadcasted_iota(jnp.int32, gain.shape, 0)
    for c in range(n_span):
        row_gains[c : c + 1] = jnp.sum(
            jnp.where(levels == step_ref[c], gain[...], 0.0), axis=0, keepdims=True
        )
    for b in range(1, n_span):
        for which in range(2):
            origin = lax.rem(span + n_span - b, n_span)
            cache_copy(which, b, origin, origin).wait_recv()
    for which, target in ((0, kd), (1, vd)):
        for e in range(n_span):

            @pl.loop(0, piece // tokens)
            def _(i, which=which, target=target, e=e):
                row = pl.multiple_of(i * tokens, tokens)
                block = cache_pairs[which][1].at[e, pl.ds(row, tokens)]
                separate(block, target, pl.multiple_of(e * piece + row, tokens))

    def window_row(slot):
        return pl.multiple_of(cached + slot * tokens, tokens)

    for kind, target in ((KEYS, kd), (VALUES, vd)):
        separate(landings[kind].at[my_slot], target, window_row(my_slot))

        @pl.loop(0, n - 1)
        def _(j, kind=kind, target=target):
            k = nth(j)
            slot = slot_of(behind(k))
            arrival(kind, k).wait_recv()
            separate(landings[kind].at[slot], target, window_row(slot))

    @pl.loop(0, n // 2)
    def _(t):
        first = lax.div(t, n_span) * 2 * n_span + lax.rem(t, n_span)
        offsets = [nth(first + i * n_span) for i in range(2)]
        block_span = behind(offsets[0])[1]
        for i, k in enumerate(offsets):
            if i == 1:

                @pl.when(k > 0)
                def _():
                    arrival(QUERIES, k).wait_recv()
            else:
                arrival(QUERIES, k).wait_recv()
            separate(qraw.at[slot_of(behind(k))], qd, i * tokens)

        for c in range(n_span):

            @pl.when(block_span == c)
            def _(c=c):
                length = cached + (c + 1) * n_seq * tokens

                @pl.loop(0, heads * members)
                def _(g):
                    scores = lax.dot_general(
                        qd[g],
                        kd[g, pl.ds(0, length), :],
                        (((1,), (1,)), ((), ())),
                        preferred_element_type=jnp.float32,
                    )
                    scores = scores * scale + bias[c : c + 1, pl.ds(0, length)]
                    largest = jnp.max(scores, axis=1, keepdims=True)
                    weights = jnp.exp(scores - largest)
                    total = jnp.sum(weights, axis=1, keepdims=True)
                    od[g] = (
                        jnp.dot(
                            weights.astype(jnp.bfloat16),
                            vd[g, pl.ds(0, length), :],
                            preferred_element_type=jnp.float32,
                        )
                        / total
                    )

                for i, k in enumerate(offsets):
                    for h in range(heads):
                        row_gain = row_gains[c : c + 1, h * HD : (h + 1) * HD]
                        for m in range(members):
                            stage[h, pl.ds(m, tokens, stride=members), :] = (
                                od[h * members + m, i * tokens : (i + 1) * tokens, :] * row_gain
                            )
                        oraw[k, :, :, h * HD : (h + 1) * HD] = (
                            stage[h].astype(jnp.bfloat16).reshape(tokens, members, HD)
                        )

        for i, k in enumerate(offsets):
            if i == 1:

                @pl.when(k > 0)
                def _():
                    give_back(k).start()
            else:
                give_back(k).start()

    last = pltpu.make_async_copy(
        oraw.at[0], out_ref.at[:, :, columns(my_group)], local_sem.at[6]
    )
    last.start()

    @pl.loop(1, n)
    def _(k):
        for kind in range(3):
            scatter(kind, k).wait_send()
        give_back(k).wait_send()
        returned(k).wait_recv()

    for b in range(1, n_span):
        for which in range(2):
            cache_copy(which, b, lax.rem(span + b, n_span), span).wait_send()
    last.wait()


def hand_over(pieces, source, target, held, in_sem, out_sem):
    rows = held.shape[0] // pieces
    parts = [pl.ds(i * rows, rows) for i in range(pieces)]
    inward = [
        pltpu.make_async_copy(source.at[part], held.at[part], in_sem.at[i])
        for i, part in enumerate(parts)
    ]
    outward = [
        pltpu.make_async_copy(held.at[part], target.at[part], out_sem.at[i])
        for i, part in enumerate(parts)
    ]
    for copy in inward:
        copy.start()
    for arriving, leaving in zip(inward, outward):
        arriving.wait()
        leaving.start()
    for copy in outward:
        copy.wait()


def per_device(
    queries,
    keys,
    values,
    cache_keys,
    cache_values,
    span_lengths,
    cache_offsets,
    step_index,
    step_gain,
):
    n_seq, n_span = lax.axis_size("seq"), lax.axis_size("span")
    n = n_seq * n_span
    tokens, members, features = queries.shape
    width = features // n
    groups = members * width // HD
    piece = cache_keys.shape[0]
    cached, span_len = n_span * piece, n_seq * tokens
    full = cached + n_span * span_len

    anywhere = pl.BlockSpec(memory_space=pl.ANY)
    scalars = pl.BlockSpec(memory_space=pltpu.SMEM)
    block = (n, tokens, members, width)
    attended = pl.pallas_call(
        functools.partial(kernel, n_seq, n_span),
        out_shape=jax.ShapeDtypeStruct(queries.shape, jnp.bfloat16),
        in_specs=[anywhere] * 5 + [scalars] * 3 + [anywhere],
        out_specs=anywhere,
        scratch_shapes=[pltpu.VMEM(block, jnp.bfloat16)] * 4
        + [pltpu.VMEM((n_span, piece, members, width), jnp.bfloat16)] * 2
        + [pltpu.VMEM((groups, full, HD), jnp.bfloat16)] * 2
        + [
            pltpu.VMEM((groups, 2 * tokens, HD), jnp.bfloat16),
            pltpu.VMEM((groups, 2 * tokens, HD), jnp.float32),
            pltpu.VMEM((width // HD, members * tokens, HD), jnp.float32),
            pltpu.VMEM((n_span, full), jnp.float32),
            pltpu.VMEM((step_gain.shape[0], width), jnp.float32),
            pltpu.VMEM((n_span, width), jnp.float32),
            pltpu.SemaphoreType.DMA((4, n)),
            pltpu.SemaphoreType.DMA((4, n)),
            pltpu.SemaphoreType.DMA((2, n_span)),
            pltpu.SemaphoreType.DMA((2, n_span)),
            pltpu.SemaphoreType.DMA((7,)),
        ],
        compiler_params=pltpu.CompilerParams(
            collective_id=0, has_side_effects=True, vmem_limit_bytes=60 * 2**20
        ),
    )(
        queries,
        keys,
        values,
        cache_keys,
        cache_values,
        span_lengths,
        cache_offsets,
        step_index,
        step_gain,
    )
    pieces = 8
    return pl.pallas_call(
        functools.partial(hand_over, pieces),
        out_shape=jax.ShapeDtypeStruct(queries.shape, jnp.bfloat16),
        in_specs=[anywhere],
        out_specs=anywhere,
        scratch_shapes=[
            pltpu.VMEM(queries.shape, jnp.bfloat16),
            pltpu.SemaphoreType.DMA((pieces,)),
            pltpu.SemaphoreType.DMA((pieces,)),
        ],
    )(attended)


def solution(mesh):
    placed = (
        P(("rep", "span", "seq"), None, None),
        P(("rep", "span", "seq"), None, None),
        P(("rep", "span", "seq"), None, None),
        P(("rep", "span"), None, "seq"),
        P(("rep", "span"), None, "seq"),
        P("rep"),
        P("rep"),
        P("rep"),
        P(),
    )
    return jax.shard_map(
        per_device,
        mesh=mesh,
        in_specs=placed,
        out_specs=P(("rep", "span", "seq"), None, None),
        check_vma=False,
    )
```

profile of v0, /device:TPU:1, one launch (start us, length us, event | category | flops | bytes accessed | tf_op | source)
XLA Modules:
  0.0 198.5 jit_solution(15378868857480783055)
XLA Ops:
  0.0 196.1 %shard_map.91.source = bf16[128,2,4096]{2,1,0:T(2,128)(2,1)} custom-call(bf16[128,2,4096]{2,1,0:T(2,128)(2,1)} %q_ref.1, bf16[128,2,4096]{2,1,0:T(2,128)(2,1)} %k_ref.1, bf16[128,2,4096]{2,1,0:T(2,128)(2,1)} %v_ref.1, bf16[256,2,512]{2,1,0:T(2,128)(2,1)} %ck_ref.1, bf16[256,2,512]{2,1,0:T(2,128)(2,1)} %cv_ref.1, s32[2]{0:T(128)} %length_ref.1, s32[2]{0:T(128)} %offset_ref.1, ...), custom_call_target="tpu_custom_call" | custom-call | tf_op jit(solution)/shard_map/pallas_call | solution.py:362
  196.1 2.4 %shard_map.92 = bf16[128,2,4096]{2,1,0:T(2,128)(2,1)} custom-call(bf16[128,2,4096]{2,1,0:T(2,128)(2,1)} %shard_map.91.source), custom_call_target="tpu_custom_call" | custom-call | tf_op jit(solution)/shard_map/pallas_call | solution.py:398
where the time goes:
time: 199 us
  Pallas kernels  199 us (100%)
    pallas_call x1, Pallas kernels, per_device(): pl.pallas_call(functools.partial(kernel, n_seq, n_span), out_shape=jax.Sh...  196 us

commit v1 on v0

--- a/solution.py
+++ b/solution.py
@@ -68,11 +68,44 @@
             lax.rem(span + n_span - lax.rem(k, n_span), n_span),
         )
 
-    def nth(j):
-        i = lax.div(j, n_span)
-        swing = lax.div(i + 1, 2) * (2 * lax.rem(i, 2) - 1)
-        lag = lax.rem(n_seq // 2 + swing + n_seq, n_seq)
-        return lag * n_span + n_span - 1 - lax.rem(j, n_span)
+    half = n_seq // 4
+    run = 2 * n_span
+    my_pair = lax.div(seq, 2)
+    upper = lax.div(my_pair, half)
+    lower = 1 - upper
+    depth = my_pair - upper * half
+    outer = lower * (1 - lax.div(depth, half - half // 2)) + upper * lax.div(depth, half // 2)
+
+    def near_pair(i):
+        return upper * half + lax.rem(depth + i, half)
+
+    def far_pair(i):
+        return lower * (2 * half - 1 - i) + upper * i
+
+    def far_target(i):
+        inwards = outer * i + (1 - outer) * (half - 1 - i)
+        return far_pair(inwards)
+
+    def near_then_far(i, far_order=far_pair):
+        far = lax.div(i, half)
+        return (1 - far) * near_pair(i) + far * far_order(i - half)
+
+    def far_then_near(i):
+        near = lax.div(i, half)
+        return near * near_pair(i - half) + (1 - near) * far_target(i)
+
+    def member_of(pair, r):
+        return (2 * pair + lax.div(r, n_span), lax.rem(r, n_span))
+
+    def lag_to(place):
+        return lax.rem(place[0] - seq + n_seq, n_seq) * n_span + lax.rem(
+            place[1] - span + n_span, n_span
+        )
+
+    def lag_from(place):
+        return lax.rem(seq - place[0] + n_seq, n_seq) * n_span + lax.rem(
+            span - place[1] + n_span, n_span
+        )
 
     def columns(group):
         return pl.ds(pl.multiple_of(group * width, HD), width)
@@ -177,11 +210,23 @@
     for b in range(1, n_span):
         for which in range(2):
             cache_copy(which, b, lax.rem(span + b, n_span), span).start()
-    for kind in range(3):
-
-        @pl.loop(0, n - 1)
-        def _(j, kind=kind):
-            scatter(kind, nth(j)).start()
+
+    def scatter_all(kind, order):
+        @pl.loop(0, n)
+        def _(j):
+            shifted = lax.rem(j + lax.rem(my_group, run), run)
+            k = lag_to(member_of(order(lax.div(j, run)), shifted))
+
+            @pl.when(k > 0)
+            def _():
+                scatter(kind, k).start()
+
+    scatter_all(KEYS, far_then_near)
+    scatter_all(VALUES, far_then_near)
+
+    @pl.when(outer == 0)
+    def _():
+        scatter_all(QUERIES, functools.partial(near_then_far, far_order=far_target))
 
     def separate(block, target, row):
         for h in range(heads):
@@ -229,27 +274,45 @@
     for kind, target in ((KEYS, kd), (VALUES, vd)):
         separate(landings[kind].at[my_slot], target, window_row(my_slot))
 
-        @pl.loop(0, n - 1)
+        @pl.loop(0, n)
         def _(j, kind=kind, target=target):
-            k = nth(j)
-            slot = slot_of(behind(k))
-            arrival(kind, k).wait_recv()
-            separate(landings[kind].at[slot], target, window_row(slot))
+            k = lag_from(member_of(near_then_far(lax.div(j, run)), lax.rem(j, run)))
+
+            @pl.when(k > 0)
+            def _():
+                slot = slot_of(behind(k))
+                arrival(kind, k).wait_recv()
+                separate(landings[kind].at[slot], target, window_row(slot))
+
+    @pl.when(outer == 1)
+    def _():
+        scatter_all(QUERIES, functools.partial(near_then_far, far_order=far_target))
+
+    def turn_lags(t):
+        pair = near_then_far(lax.div(t, n_span))
+        block_span = lax.rem(t, n_span)
+        return [lag_from((2 * pair + i, block_span)) for i in range(2)]
+
+    last_pair = n // 2 - n_span
 
     @pl.loop(0, n // 2)
     def _(t):
-        first = lax.div(t, n_span) * 2 * n_span + lax.rem(t, n_span)
-        offsets = [nth(first + i * n_span) for i in range(2)]
-        block_span = behind(offsets[0])[1]
+        offsets = turn_lags(t)
+        block_span = lax.rem(t, n_span)
         for i, k in enumerate(offsets):
-            if i == 1:
-
-                @pl.when(k > 0)
-                def _():
-                    arrival(QUERIES, k).wait_recv()
-            else:
+
+            @pl.when(k > 0)
+            def _(k=k):
                 arrival(QUERIES, k).wait_recv()
+
             separate(qraw.at[slot_of(behind(k))], qd, i * tokens)
+
+        @pl.when((outer == 1) & (t == last_pair))
+        def _():
+            @pl.loop(half * n_span, last_pair)
+            def _(earlier):
+                for k in turn_lags(earlier):
+                    give_back(k).start()
 
         for c in range(n_span):
 
@@ -289,13 +352,11 @@
                             stage[h].astype(jnp.bfloat16).reshape(tokens, members, HD)
                         )
 
-        for i, k in enumerate(offsets):
-            if i == 1:
-
-                @pl.when(k > 0)
-                def _():
-                    give_back(k).start()
-            else:
+        held_back = (outer == 1) & (t >= half * n_span) & (t < last_pair)
+        for k in offsets:
+
+            @pl.when((k > 0) & jnp.logical_not(held_back))
+            def _(k=k):
                 give_back(k).start()
 
     last = pltpu.make_async_copy(

time: 199 us -> 192 us (0.965)
  the two profiles are of different devices: /device:TPU:1 before, /device:TPU:13 now
where the time goes in v1:
time: 192 us
  Pallas kernels  192 us (100%)
    pallas_call x1, Pallas kernels, per_device(): pl.pallas_call(functools.partial(kernel, n_seq, n_span), out_shape=jax.Sh...  189 us

profile of v1, /device:TPU:13, one launch (start us, length us, event | category | flops | bytes accessed | tf_op | source)
XLA Modules:
  0.0 191.8 jit_solution(8132705973478508516)
XLA Ops:
  0.0 189.4 %shard_map.91.source = bf16[128,2,4096]{2,1,0:T(2,128)(2,1)} custom-call(bf16[128,2,4096]{2,1,0:T(2,128)(2,1)} %q_ref.1, bf16[128,2,4096]{2,1,0:T(2,128)(2,1)} %k_ref.1, bf16[128,2,4096]{2,1,0:T(2,128)(2,1)} %v_ref.1, bf16[256,2,512]{2,1,0:T(2,128)(2,1)} %ck_ref.1, bf16[256,2,512]{2,1,0:T(2,128)(2,1)} %cv_ref.1, s32[2]{0:T(128)} %length_ref.1, s32[2]{0:T(128)} %offset_ref.1, ...), custom_call_target="tpu_custom_call" | custom-call | tf_op jit(solution)/shard_map/pallas_call | solution.py:423
  189.4 2.4 %shard_map.92 = bf16[128,2,4096]{2,1,0:T(2,128)(2,1)} custom-call(bf16[128,2,4096]{2,1,0:T(2,128)(2,1)} %shard_map.91.source), custom_call_target="tpu_custom_call" | custom-call | tf_op jit(solution)/shard_map/pallas_call | solution.py:459

commit v2 on v1

--- a/solution.py
+++ b/solution.py
@@ -42,6 +42,7 @@
     row_gains,
     send_sem,
     recv_sem,
+    back_sem,
     cache_send,
     cache_recv,
     local_sem,
@@ -82,25 +83,12 @@
     def far_pair(i):
         return lower * (2 * half - 1 - i) + upper * i
 
-    def far_target(i):
-        inwards = outer * i + (1 - outer) * (half - 1 - i)
-        return far_pair(inwards)
-
-    def near_then_far(i, far_order=far_pair):
+    def near_then_far(i):
         far = lax.div(i, half)
-        return (1 - far) * near_pair(i) + far * far_order(i - half)
-
-    def far_then_near(i):
-        near = lax.div(i, half)
-        return near * near_pair(i - half) + (1 - near) * far_target(i)
+        return (1 - far) * near_pair(i) + far * far_pair(i - half)
 
     def member_of(pair, r):
         return (2 * pair + lax.div(r, n_span), lax.rem(r, n_span))
-
-    def lag_to(place):
-        return lax.rem(place[0] - seq + n_seq, n_seq) * n_span + lax.rem(
-            place[1] - span + n_span, n_span
-        )
 
     def lag_from(place):
         return lax.rem(seq - place[0] + n_seq, n_seq) * n_span + lax.rem(
@@ -122,47 +110,37 @@
     sources = (k_ref, v_ref, q_ref)
     landings = (kraw, vraw, qraw)
 
-    def scatter(kind, k):
-        to = ahead(k)
+    def scatter(kind, to):
         return pltpu.make_async_remote_copy(
             src_ref=sources[kind].at[:, :, columns(group_of(to))],
             dst_ref=landings[kind].at[my_slot],
-            send_sem=send_sem.at[kind, k],
-            recv_sem=recv_sem.at[kind, k],
+            send_sem=send_sem.at[kind],
+            recv_sem=recv_sem.at[kind, my_pair],
             device_id=device(to),
             device_id_type=MESH,
         )
 
-    def arrival(kind, k):
-        origin = behind(k)
-        return pltpu.make_async_remote_copy(
-            src_ref=sources[kind].at[:, :, columns(group_of(origin))],
-            dst_ref=landings[kind].at[slot_of(origin)],
-            send_sem=send_sem.at[kind, k],
-            recv_sem=recv_sem.at[kind, k],
-            device_id=device(origin),
-            device_id_type=MESH,
-        )
+    def take(blocks, sem):
+        many = kraw.at[pl.ds(0, blocks)]
+        pltpu.make_async_copy(many, many, sem).wait()
+
+    def arrival(kind, i, pair):
+        @pl.when(i == 0)
+        def _():
+            take(run - 1, recv_sem.at[kind, pair])
+
+        @pl.when(i > 0)
+        def _():
+            take(run, recv_sem.at[kind, pair])
 
     def give_back(k):
         to = behind(k)
         return pltpu.make_async_remote_copy(
             src_ref=oraw.at[k],
             dst_ref=out_ref.at[:, :, columns(my_group)],
-            send_sem=send_sem.at[OUTS, k],
-            recv_sem=recv_sem.at[OUTS, k],
+            send_sem=send_sem.at[OUTS],
+            recv_sem=back_sem,
             device_id=device(to),
-            device_id_type=MESH,
-        )
-
-    def returned(k):
-        origin = ahead(k)
-        return pltpu.make_async_remote_copy(
-            src_ref=oraw.at[k],
-            dst_ref=out_ref.at[:, :, columns(group_of(origin))],
-            send_sem=send_sem.at[OUTS, k],
-            recv_sem=recv_sem.at[OUTS, k],
-            device_id=device(origin),
             device_id_type=MESH,
         )
 
@@ -173,8 +151,8 @@
         return pltpu.make_async_remote_copy(
             src_ref=source.at[:, :, columns(to_span)],
             dst_ref=landing.at[from_span],
-            send_sem=cache_send.at[which, b],
-            recv_sem=cache_recv.at[which, b],
+            send_sem=cache_send.at[which, b - 1],
+            recv_sem=cache_recv.at[which, b - 1],
             device_id={"span": to_span},
             device_id_type=MESH,
         )
@@ -199,8 +177,7 @@
 
     barrier = pltpu.get_barrier_semaphore()
 
-    @pl.loop(1, n)
-    def _(k):
+    for k in range(1, n):
         pl.semaphore_signal(barrier, inc=1, device_id=device(ahead(k)), device_id_type=MESH)
 
     for copy in own_copies:
@@ -211,22 +188,32 @@
         for which in range(2):
             cache_copy(which, b, lax.rem(span + b, n_span), span).start()
 
-    def scatter_all(kind, order):
-        @pl.loop(0, n)
-        def _(j):
-            shifted = lax.rem(j + lax.rem(my_group, run), run)
-            k = lag_to(member_of(order(lax.div(j, run)), shifted))
-
-            @pl.when(k > 0)
-            def _():
-                scatter(kind, k).start()
-
-    scatter_all(KEYS, far_then_near)
-    scatter_all(VALUES, far_then_near)
+    flips = {
+        1 << b: (1 << b) * (1 - 2 * lax.rem(lax.div(my_group, 1 << b), 2))
+        for b in range(n.bit_length() - 1)
+    }
+
+    def across(mask):
+        group = my_group + sum(flip for bit, flip in flips.items() if mask & bit)
+        return lax.div(group, n_span), lax.rem(group, n_span)
+
+    far_masks = [n // 2 + (i % 2) * (n // 4) + i // 2 for i in range(n // 2)]
+    near_masks = list(range(n // 4, n // 2)) + list(range(1, n // 4))
+
+    def scatter_all(kind, masks):
+        for mask in masks:
+            scatter(kind, across(mask)).start()
+
+    alternating = far_masks[:1]
+    for pair in zip(near_masks, far_masks[1:]):
+        alternating += pair
+    scatter_all(KEYS, alternating)
+    scatter_all(VALUES, alternating)
+    scatter_all(QUERIES, near_masks)
 
     @pl.when(outer == 0)
     def _():
-        scatter_all(QUERIES, functools.partial(near_then_far, far_order=far_target))
+        scatter_all(QUERIES, far_masks)
 
     def separate(block, target, row):
         for h in range(heads):
@@ -272,39 +259,39 @@
         return pl.multiple_of(cached + slot * tokens, tokens)
 
     for kind, target in ((KEYS, kd), (VALUES, vd)):
-        separate(landings[kind].at[my_slot], target, window_row(my_slot))
-
-        @pl.loop(0, n)
-        def _(j, kind=kind, target=target):
-            k = lag_from(member_of(near_then_far(lax.div(j, run)), lax.rem(j, run)))
-
-            @pl.when(k > 0)
-            def _():
-                slot = slot_of(behind(k))
-                arrival(kind, k).wait_recv()
+
+        @pl.loop(0, 2 * half)
+        def _(i, kind=kind, target=target):
+            pair = near_then_far(i)
+            arrival(kind, i, pair)
+
+            @pl.loop(0, run)
+            def _(r):
+                slot = slot_of(member_of(pair, r))
                 separate(landings[kind].at[slot], target, window_row(slot))
 
     @pl.when(outer == 1)
     def _():
-        scatter_all(QUERIES, functools.partial(near_then_far, far_order=far_target))
+        scatter_all(QUERIES, far_masks)
 
     def turn_lags(t):
         pair = near_then_far(lax.div(t, n_span))
-        block_span = lax.rem(t, n_span)
-        return [lag_from((2 * pair + i, block_span)) for i in range(2)]
+        block_span = lax.rem(t + span, n_span)
+        return [lag_from((2 * pair + lax.rem(i + seq, 2), block_span)) for i in range(2)]
 
     last_pair = n // 2 - n_span
 
     @pl.loop(0, n // 2)
     def _(t):
         offsets = turn_lags(t)
-        block_span = lax.rem(t, n_span)
+        block_span = lax.rem(t + span, n_span)
+
+        @pl.when(lax.rem(t, n_span) == 0)
+        def _():
+            i = lax.div(t, n_span)
+            arrival(QUERIES, i, near_then_far(i))
+
         for i, k in enumerate(offsets):
-
-            @pl.when(k > 0)
-            def _(k=k):
-                arrival(QUERIES, k).wait_recv()
-
             separate(qraw.at[slot_of(behind(k))], qd, i * tokens)
 
         @pl.when((outer == 1) & (t == last_pair))
@@ -364,12 +351,9 @@
     )
     last.start()
 
-    @pl.loop(1, n)
-    def _(k):
-        for kind in range(3):
-            scatter(kind, k).wait_send()
-        give_back(k).wait_send()
-        returned(k).wait_recv()
+    for kind in range(4):
+        take(n - 1, send_sem.at[kind])
+    take(n - 1, back_sem)
 
     for b in range(1, n_span):
         for which in range(2):
@@ -377,22 +361,16 @@
     last.wait()
 
 
-def hand_over(pieces, source, target, held, in_sem, out_sem):
-    rows = held.shape[0] // pieces
-    parts = [pl.ds(i * rows, rows) for i in range(pieces)]
-    inward = [
-        pltpu.make_async_copy(source.at[part], held.at[part], in_sem.at[i])
-        for i, part in enumerate(parts)
+def hand_over(pieces, source, target, sem):
+    rows = source.shape[0] // pieces
+    outward = [
+        pltpu.make_async_copy(
+            source.at[pl.ds(i * rows, rows)], target.at[pl.ds(i * rows, rows)], sem.at[i]
+        )
+        for i in range(pieces)
     ]
-    outward = [
-        pltpu.make_async_copy(held.at[part], target.at[part], out_sem.at[i])
-        for i, part in enumerate(parts)
-    ]
-    for copy in inward:
+    for copy in outward:
         copy.start()
-    for arriving, leaving in zip(inward, outward):
-        arriving.wait()
-        leaving.start()
     for copy in outward:
         copy.wait()
 
@@ -422,9 +400,9 @@
     block = (n, tokens, members, width)
     attended = pl.pallas_call(
         functools.partial(kernel, n_seq, n_span),
-        out_shape=jax.ShapeDtypeStruct(queries.shape, jnp.bfloat16),
+        out_shape=pltpu.VMEM(queries.shape, jnp.bfloat16),
         in_specs=[anywhere] * 5 + [scalars] * 3 + [anywhere],
-        out_specs=anywhere,
+        out_specs=pl.BlockSpec(memory_space=pltpu.VMEM),
         scratch_shapes=[pltpu.VMEM(block, jnp.bfloat16)] * 4
         + [pltpu.VMEM((n_span, piece, members, width), jnp.bfloat16)] * 2
         + [pltpu.VMEM((groups, full, HD), jnp.bfloat16)] * 2
@@ -435,10 +413,11 @@
             pltpu.VMEM((n_span, full), jnp.float32),
             pltpu.VMEM((step_gain.shape[0], width), jnp.float32),
             pltpu.VMEM((n_span, width), jnp.float32),
-            pltpu.SemaphoreType.DMA((4, n)),
-            pltpu.SemaphoreType.DMA((4, n)),
-            pltpu.SemaphoreType.DMA((2, n_span)),
-            pltpu.SemaphoreType.DMA((2, n_span)),
+            pltpu.SemaphoreType.DMA((4,)),
+            pltpu.SemaphoreType.DMA((3, n_seq // 2)),
+            pltpu.SemaphoreType.DMA,
+            pltpu.SemaphoreType.DMA((2, n_span - 1)),
+            pltpu.SemaphoreType.DMA((2, n_span - 1)),
             pltpu.SemaphoreType.DMA((7,)),
         ],
         compiler_params=pltpu.CompilerParams(
@@ -455,17 +434,14 @@
         step_index,
         step_gain,
     )
-    pieces = 8
+    pieces = 4
     return pl.pallas_call(
         functools.partial(hand_over, pieces),
         out_shape=jax.ShapeDtypeStruct(queries.shape, jnp.bfloat16),
-        in_specs=[anywhere],
+        in_specs=[pl.BlockSpec(memory_space=pltpu.VMEM)],
         out_specs=anywhere,
-        scratch_shapes=[
-            pltpu.VMEM(queries.shape, jnp.bfloat16),
-            pltpu.SemaphoreType.DMA((pieces,)),
-            pltpu.SemaphoreType.DMA((pieces,)),
-        ],
+        scratch_shapes=[pltpu.SemaphoreType.DMA((pieces,))],
+        compiler_params=pltpu.CompilerParams(vmem_limit_bytes=16 * 2**20),
     )(attended)
 
 

time: 192 us -> 188 us (0.979)
  Pallas kernels: 192 us -> 188 us
    pallas_call x1, Pallas kernels: 189 us -> 187 us  [per_device(): pl.pallas_call(functools.partial(kernel, n_seq, n_span), out_shape=pltpu....]
where the time goes in v2:
time: 188 us
  Pallas kernels  188 us (100%)
    pallas_call x1, Pallas kernels, per_device(): pl.pallas_call(functools.partial(kernel, n_seq, n_span), out_shape=pltpu....  187 us

profile of v2, /device:TPU:13, one launch (start us, length us, event | category | flops | bytes accessed | tf_op | source)
XLA Modules:
  0.0 188.0 jit_solution(14882412881388803184)
XLA Ops:
  0.0 186.7 %shard_map.91.source = bf16[128,2,4096]{2,1,0:T(2,128)(2,1)S(1)} custom-call(bf16[128,2,4096]{2,1,0:T(2,128)(2,1)} %q_ref.1, bf16[128,2,4096]{2,1,0:T(2,128)(2,1)} %k_ref.1, bf16[128,2,4096]{2,1,0:T(2,128)(2,1)} %v_ref.1, bf16[256,2,512]{2,1,0:T(2,128)(2,1)} %ck_ref.1, bf16[256,2,512]{2,1,0:T(2,128)(2,1)} %cv_ref.1, s32[2]{0:T(128)} %length_ref.1, ...), custom_call_target="tpu_custom_call" | custom-call | tf_op jit(solution)/shard_map/pallas_call | solution.py:401
  186.7 1.3 shard_map.92

commit v3 on v2

--- a/solution.py
+++ b/solution.py
@@ -46,6 +46,7 @@
     cache_send,
     cache_recv,
     local_sem,
+    late_sem,
 ):
     n = n_seq * n_span
     seq, span = lax.axis_index("seq"), lax.axis_index("span")
@@ -177,17 +178,6 @@
 
     barrier = pltpu.get_barrier_semaphore()
 
-    for k in range(1, n):
-        pl.semaphore_signal(barrier, inc=1, device_id=device(ahead(k)), device_id_type=MESH)
-
-    for copy in own_copies:
-        copy.start()
-    pl.semaphore_wait(barrier, n - 1)
-
-    for b in range(1, n_span):
-        for which in range(2):
-            cache_copy(which, b, lax.rem(span + b, n_span), span).start()
-
     flips = {
         1 << b: (1 << b) * (1 - 2 * lax.rem(lax.div(my_group, 1 << b), 2))
         for b in range(n.bit_length() - 1)
@@ -197,6 +187,42 @@
         group = my_group + sum(flip for bit, flip in flips.items() if mask & bit)
         return lax.div(group, n_span), lax.rem(group, n_span)
 
+    def greet(masks, sem):
+        for mask in masks:
+            pl.semaphore_signal(
+                sem, inc=1, device_id=device(across(mask)), device_id_type=MESH
+            )
+
+    alike = list(range(3 * n // 4, n)) + list(range(1, n // 4))
+    unlike = list(range(n // 4, 3 * n // 4))
+    early = alike[:1]
+
+    @pl.when(outer == 0)
+    def _():
+        greet(unlike, barrier)
+
+    greet(alike, barrier)
+    for copy in own_copies:
+        copy.start()
+
+    @pl.when(outer == 0)
+    def _():
+        pl.semaphore_wait(barrier, len(alike))
+        for mask in early:
+            scatter(KEYS, across(mask)).start()
+        pl.semaphore_wait(late_sem, len(unlike))
+
+    @pl.when(outer == 1)
+    def _():
+        pl.semaphore_wait(barrier, n - 1)
+        greet(unlike, late_sem)
+        for mask in early:
+            scatter(KEYS, across(mask)).start()
+
+    for b in range(1, n_span):
+        for which in range(2):
+            cache_copy(which, b, lax.rem(span + b, n_span), span).start()
+
     far_masks = [n // 2 + (i % 2) * (n // 4) + i // 2 for i in range(n // 2)]
     near_masks = list(range(n // 4, n // 2)) + list(range(1, n // 4))
 
@@ -207,7 +233,7 @@
     alternating = far_masks[:1]
     for pair in zip(near_masks, far_masks[1:]):
         alternating += pair
-    scatter_all(KEYS, alternating)
+    scatter_all(KEYS, [mask for mask in alternating if mask not in early])
     scatter_all(VALUES, alternating)
     scatter_all(QUERIES, near_masks)
 
@@ -276,15 +302,15 @@
 
     def turn_lags(t):
         pair = near_then_far(lax.div(t, n_span))
-        block_span = lax.rem(t + span, n_span)
-        return [lag_from((2 * pair + lax.rem(i + seq, 2), block_span)) for i in range(2)]
+        block_span = lax.rem(t, n_span)
+        return [lag_from((2 * pair + i, block_span)) for i in range(2)]
 
     last_pair = n // 2 - n_span
 
     @pl.loop(0, n // 2)
     def _(t):
         offsets = turn_lags(t)
-        block_span = lax.rem(t + span, n_span)
+        block_span = lax.rem(t, n_span)
 
         @pl.when(lax.rem(t, n_span) == 0)
         def _():
@@ -419,6 +445,7 @@
             pltpu.SemaphoreType.DMA((2, n_span - 1)),
             pltpu.SemaphoreType.DMA((2, n_span - 1)),
             pltpu.SemaphoreType.DMA((7,)),
+            pltpu.SemaphoreType.REGULAR,
         ],
         compiler_params=pltpu.CompilerParams(
             collective_id=0, has_side_effects=True, vmem_limit_bytes=60 * 2**20

time: 188 us -> 187 us (level)
  no operation moved by 1% of the time
where the time goes in v3:
time: 187 us
  Pallas kernels  187 us (100%)
    pallas_call x1, Pallas kernels, per_device(): pl.pallas_call(functools.partial(kernel, n_seq, n_span), out_shape=pltpu....  186 us

profile of v3, /device:TPU:13, one launch (start us, length us, event | category | flops | bytes accessed | tf_op | source)
XLA Modules:
  0.0 187.0 jit_solution(10268830034612736561)
XLA Ops:
  0.0 185.6 %shard_map.91.source = bf16[128,2,4096]{2,1,0:T(2,128)(2,1)S(1)} custom-call(bf16[128,2,4096]{2,1,0:T(2,128)(2,1)} %q_ref.1, bf16[128,2,4096]{2,1,0:T(2,128)(2,1)} %k_ref.1, bf16[128,2,4096]{2,1,0:T(2,128)(2,1)} %v_ref.1, bf16[256,2,512]{2,1,0:T(2,128)(2,1)} %ck_ref.1, bf16[256,2,512]{2,1,0:T(2,128)(2,1)} %cv_ref.1, s32[2]{0:T(128)} %length_ref.1, ...), custom_call_target="tpu_custom_call" | custom-call | tf_op jit(solution)/shard_map/pallas_call | solution.py:427
  185.6 1.3 shard_map.92
